TPU v7x, 32 devices: a whole 2x2x4 slice. The times are simulated.
32 devices in a mesh: tm: 4 (over x, core), space: 8 (over z, y).
Axes of the slice: x: 2, y: 2, z: 4, core: 2. Of those that a mesh axis runs over, the one named last changes fastest.
Arguments:
- state_rhs: float32 [32, 16, 128, 128], P('tm', 'space'), may hold values from -5 to 9
- adjoint_rhs: float32 [32, 16, 128, 128], P('tm', 'space'), may hold values from -5 to 9
- reaction: float32 [16, 128, 128], P('space'), may hold values from 0.01 to 1
Outputs:
- state_out: float32 [32, 16, 128, 128], P('tm', 'space')
- adjoint_out: float32 [32, 16, 128, 128], P('tm', 'space')
All inputs are finite; a program needn't handle non-finite values.
Results may differ from a plain program's by a relative error of at most 0.00021.
Values sent between devices are 32-bit elements; how exact they have to be, the bound alone decides.
A program may use at most 64 MiB of HBM per device.

v0:
```python
import math

import jax
import jax.numpy as jnp
from jax import lax
from jax.sharding import PartitionSpec as P

STEPS = 32
SWEEPS = 12


ALPHA = 0.1
MU = 1.0
BETA = 1.0


def padded_2(cells, sides, width):
    for axis, dim in sides:
        count = lax.axis_size(axis)
        ends = count - 1
        head = lax.slice_in_dim(cells, 0, width, axis=dim)
        tail = lax.slice_in_dim(cells, cells.shape[dim] - width, cells.shape[dim], axis=dim)
        cells = jnp.concatenate(
            [
                lax.ppermute(tail, axis, [(i, (i + 1) % count) for i in range(ends)]),
                cells,
                lax.ppermute(head, axis, [((i + 1) % count, i) for i in range(ends)]),
            ],
            axis=dim,
        )
    return cells


def coefficients(reaction, freqs):
    turn = 2.0 * math.pi * freqs.astype(jnp.float32) / STEPS
    rate = math.exp(math.log(ALPHA) / STEPS)
    lam_re = 1.0 - rate * jnp.cos(turn)
    lam_im = rate * jnp.sin(turn)
    shaped = (-1,) + (1,) * reaction.ndim
    d_re = lam_re.reshape(shaped) + MU * (6.0 + reaction)
    d_im = jnp.broadcast_to(lam_im.reshape(shaped), d_re.shape)
    den_re = d_re * d_re - d_im * d_im + BETA * BETA
    den_im = 2.0 * d_re * d_im
    magnitude = den_re * den_re + den_im * den_im
    inv_re = den_re / magnitude
    inv_im = -den_im / magnitude
    return (
        d_re * inv_re - d_im * inv_im,
        d_re * inv_im + d_im * inv_re,
        BETA * inv_re,
        BETA * inv_im,
    )


def block_solve(coefficient, source):
    q_re, q_im, r_re, r_im = coefficient
    y_real = source[..., 0, :, :, :]
    y_imag = source[..., 1, :, :, :]
    p_real = source[..., 2, :, :, :]
    p_imag = source[..., 3, :, :, :]
    new_yre = q_re * y_real - q_im * y_imag + (r_re * p_real - r_im * p_imag)
    new_yim = q_re * y_imag + q_im * y_real + (r_re * p_imag + r_im * p_real)
    new_pre = q_re * p_real - q_im * p_imag - (r_re * y_real - r_im * y_imag)
    new_pim = q_re * p_imag + q_im * p_real - (r_re * y_imag + r_im * y_real)
    return jnp.stack((new_yre, new_yim, new_pre, new_pim), axis=-4)


def neighbour_sum(zpadded):
    inner = zpadded[:, :, 1:-1]
    padded = jnp.pad(inner, ((0, 0), (0, 0), (0, 0), (1, 1), (1, 1)))
    total = zpadded[:, :, 2:] + zpadded[:, :, :-2]
    total = total + padded[:, :, :, 2:, 1:-1] + padded[:, :, :, :-2, 1:-1]
    return total + padded[:, :, :, 1:-1, 2:] + padded[:, :, :, 1:-1, :-2]


def effective(times, reverse):
    if reverse:
        return STEPS - 1 - times
    return times


def forward_table(freqs, times, reverse):
    moment = effective(times, reverse)
    phase = freqs[:, None] * moment[None, :] % STEPS
    angle = 2.0 * math.pi / STEPS * phase.astype(jnp.float32)
    growth = jnp.exp(math.log(ALPHA) * moment.astype(jnp.float32) / STEPS)[None, :]
    table = jnp.stack((jnp.cos(angle) * growth, -jnp.sin(angle) * growth), axis=1)
    return table.reshape(-1, times.shape[0])


def inverse_table(freqs, times, reverse):
    moment = effective(times, reverse)
    phase = moment[:, None] * freqs[None, :] % STEPS
    angle = 2.0 * math.pi / STEPS * phase.astype(jnp.float32)
    shrink = jnp.exp(-math.log(ALPHA) * moment.astype(jnp.float32) / STEPS)[:, None] / STEPS
    table = jnp.stack((jnp.cos(angle) * shrink, -jnp.sin(angle) * shrink), axis=2)
    return table.reshape(times.shape[0], -1)


def forward_pair(state_part, adjoint_part, freqs, times):
    rows = state_part.shape[0]
    state_hat = jnp.dot(
        forward_table(freqs, times, False),
        state_part.reshape(rows, -1),
        precision=lax.Precision.HIGHEST,
    )
    adjoint_hat = jnp.dot(
        forward_table(freqs, times, True),
        adjoint_part.reshape(rows, -1),
        precision=lax.Precision.HIGHEST,
    )
    return (state_hat, adjoint_hat)


def backward_pair(solved, freqs, times):
    count = solved.shape[0]
    slab = solved.shape[2:]
    flat_state = solved[:, 0:2].reshape(2 * count, -1)
    flat_adjoint = solved[:, 2:4].reshape(2 * count, -1)
    state_time = jnp.dot(
        inverse_table(freqs, times, False), flat_state, precision=lax.Precision.HIGHEST
    )
    adjoint_time = jnp.dot(
        inverse_table(freqs, times, True), flat_adjoint, precision=lax.Precision.HIGHEST
    )
    shaped = (times.shape[0],) + slab
    return (state_time.reshape(shaped), adjoint_time.reshape(shaped))


def body(state_rhs, adjoint_rhs, reaction):
    groups = lax.axis_size("tm")
    local_steps = state_rhs.shape[0]
    freq_count = STEPS // groups
    slab_shape = state_rhs.shape[1:]
    freqs = lax.axis_index("tm") * freq_count + jnp.arange(freq_count, dtype=jnp.int32)
    pieces = (
        lax.all_gather(state_rhs, "tm", axis=0, tiled=True),
        lax.all_gather(adjoint_rhs, "tm", axis=0, tiled=True),
    )
    rows = pieces[0].shape[0]
    times = jnp.arange(rows, dtype=jnp.int32)
    state_hat, adjoint_hat = forward_pair(pieces[0], pieces[1], freqs, times)
    state_hat, adjoint_hat = (state_hat, adjoint_hat)
    sources = jnp.concatenate(
        (
            state_hat.reshape((freq_count, 2) + slab_shape),
            adjoint_hat.reshape((freq_count, 2) + slab_shape),
        ),
        axis=1,
    )
    coefficient = coefficients(reaction, freqs)
    field = block_solve(coefficient, sources)

    def sweep(sweep_index, current):
        zpadded = padded_2(current, (("space", 2),), 1)
        return block_solve(coefficient, sources + MU * neighbour_sum(zpadded))

    solved = lax.fori_loop(0, SWEEPS - 1, sweep, field)
    times = jnp.arange(local_steps * lax.axis_size("tm"), dtype=jnp.int32)
    state_time, adjoint_time = backward_pair(solved, freqs, times)
    combined = lax.psum_scatter(
        jnp.stack((state_time, adjoint_time), axis=1), "tm", scatter_dimension=0, tiled=True
    )
    state_out = combined[:, 0]
    adjoint_out = combined[:, 1]
    return (state_out, adjoint_out)


def solution(mesh):
    in_specs = (P("tm", "space", None, None), P("tm", "space", None, None), P("space", None, None))
    out_specs = (P("tm", "space", None, None), P("tm", "space", None, None))
    return jax.shard_map(body, mesh=mesh, in_specs=in_specs, out_specs=out_specs, check_vma=False)
```

profile of v0, /device:TPU:0, one launch (start us, length us, event | category | flops | bytes accessed | tf_op | source)
XLA Modules:
  0.0 1493.0 jit_solution(3782043023437946027)
XLA Ops:
  10.1 36.7 %all-gather.5.cloned.1.call-done = f32[32,2,128,128]{3,2,1,0:T(8,128)} async-done(((f32[8,2,128,128]{3,2,1,0:T(8,128)}), f32[32,2,128,128]{3,2,1,0:T(8,128)}) %all-gather.5.cloned.1.call-update) | async-done | bytes 4194320 | tf_op jit(solution)/shard_map/all_gather | solution.py:138
  46.7 4.6 copy.67
  54.1 28.7 %all-gather.3.cloned.1.call-done = f32[32,2,128,128]{3,2,1,0:T(8,128)} async-done(((f32[8,2,128,128]{3,2,1,0:T(8,128)}), f32[32,2,128,128]{3,2,1,0:T(8,128)}) %all-gather.3.cloned.1.call-update) | async-done | bytes 4194320 | tf_op jit(solution)/shard_map/all_gather | solution.py:137
  82.8 4.6 copy.68
  89.6 4.4 fusion.34
  94.0 14.5 fusion.36
  116.8 1226.4 %while.14 = (s32[]{:T(128)}, f32[8,4,2,128,128]{4,3,2,1,0:T(8,128)}, f32[8,4,2,128,128]{4,3,2,1,0:T(8,128)}, f32[8]{0:T(128)S(1)}, f32[2,128,128]{2,1,0:T(8,128)...) while((s32[]{:T(128)}, f32[8,4,2,128,128]{4,3,2,1,0:T(8,128)}, ...), condition=%wide.region_1.2_spmd.clone.clone, body=%wide.region_0.1_spmd.clone.clone.sunk | while | flops 27787264 | bytes 63177132 | solution.py:158
  120.8 4.8 collective-permute-start
  126.8 87.8 %collective-permute-done = f32[8,4,1,128,128]{4,3,2,1,0:T(8,128)} collective-permute-done((f32[8,4,1,128,128]{4,3,2,1,0:T(8,128)}, f32[8,4,1,128,128]{4,3,2,1,0:T(8,128)}, u32[]{:S(2)}, u32[]{:S(2)}) %collective-permute-start) | collective-permute-done | bytes 2097184 | tf_op jit(solution)/shard_map/while/body/eval_jaxpr/ppermute | solution.py:25
  214.7 11.2 fusion.87
  234.5 5.8 collective-permute-start
  241.5 87.0 %collective-permute-done = f32[8,4,1,128,128]{4,3,2,1,0:T(8,128)} collective-permute-done((f32[8,4,1,128,128]{4,3,2,1,0:T(8,128)}, f32[8,4,1,128,128]{4,3,2,1,0:T(8,128)}, u32[]{:S(2)}, u32[]{:S(2)}) %collective-permute-start) | collective-permute-done | bytes 2097184 | tf_op jit(solution)/shard_map/while/body/eval_jaxpr/ppermute | solution.py:25
  328.5 11.2 fusion.87
  348.3 5.8 collective-permute-start
  355.4 86.1 %collective-permute-done = f32[8,4,1,128,128]{4,3,2,1,0:T(8,128)} collective-permute-done((f32[8,4,1,128,128]{4,3,2,1,0:T(8,128)}, f32[8,4,1,128,128]{4,3,2,1,0:T(8,128)}, u32[]{:S(2)}, u32[]{:S(2)}) %collective-permute-start) | collective-permute-done | bytes 2097184 | tf_op jit(solution)/shard_map/while/body/eval_jaxpr/ppermute | solution.py:25
  441.5 11.2 fusion.87
  461.3 5.8 collective-permute-start
  468.4 85.3 %collective-permute-done = f32[8,4,1,128,128]{4,3,2,1,0:T(8,128)} collective-permute-done((f32[8,4,1,128,128]{4,3,2,1,0:T(8,128)}, f32[8,4,1,128,128]{4,3,2,1,0:T(8,128)}, u32[]{:S(2)}, u32[]{:S(2)}) %collective-permute-start) | collective-permute-done | bytes 2097184 | tf_op jit(solution)/shard_map/while/body/eval_jaxpr/ppermute | solution.py:25
  553.7 11.2 fusion.87
  573.5 5.8 collective-permute-start
  580.5 84.4 %collective-permute-done = f32[8,4,1,128,128]{4,3,2,1,0:T(8,128)} collective-permute-done((f32[8,4,1,128,128]{4,3,2,1,0:T(8,128)}, f32[8,4,1,128,128]{4,3,2,1,0:T(8,128)}, u32[]{:S(2)}, u32[]{:S(2)}) %collective-permute-start) | collective-permute-done | bytes 2097184 | tf_op jit(solution)/shard_map/while/body/eval_jaxpr/ppermute | solution.py:25
  665.0 11.2 fusion.87
  684.8 5.8 collective-permute-start
  691.8 83.6 %collective-permute-done = f32[8,4,1,128,128]{4,3,2,1,0:T(8,128)} collective-permute-done((f32[8,4,1,128,128]{4,3,2,1,0:T(8,128)}, f32[8,4,1,128,128]{4,3,2,1,0:T(8,128)}, u32[]{:S(2)}, u32[]{:S(2)}) %collective-permute-start) | collective-permute-done | bytes 2097184 | tf_op jit(solution)/shard_map/while/body/eval_jaxpr/ppermute | solution.py:25
  775.4 11.2 fusion.87
  795.2 5.8 collective-permute-start
  802.3 82.7 %collective-permute-done = f32[8,4,1,128,128]{4,3,2,1,0:T(8,128)} collective-permute-done((f32[8,4,1,128,128]{4,3,2,1,0:T(8,128)}, f32[8,4,1,128,128]{4,3,2,1,0:T(8,128)}, u32[]{:S(2)}, u32[]{:S(2)}) %collective-permute-start) | collective-permute-done | bytes 2097184 | tf_op jit(solution)/shard_map/while/body/eval_jaxpr/ppermute | solution.py:25
  885.0 11.2 fusion.87
  900.8 4.0 fusion.86
  904.8 5.8 collective-permute-start
  911.8 81.9 %collective-permute-done = f32[8,4,1,128,128]{4,3,2,1,0:T(8,128)} collective-permute-done((f32[8,4,1,128,128]{4,3,2,1,0:T(8,128)}, f32[8,4,1,128,128]{4,3,2,1,0:T(8,128)}, u32[]{:S(2)}, u32[]{:S(2)}) %collective-permute-start) | collective-permute-done | bytes 2097184 | tf_op jit(solution)/shard_map/while/body/eval_jaxpr/ppermute | solution.py:25
  993.7 11.2 fusion.87
  1013.5 5.8 collective-permute-start
  1020.6 81.0 %collective-permute-done = f32[8,4,1,128,128]{4,3,2,1,0:T(8,128)} collective-permute-done((f32[8,4,1,128,128]{4,3,2,1,0:T(8,128)}, f32[8,4,1,128,128]{4,3,2,1,0:T(8,128)}, u32[]{:S(2)}, u32[]{:S(2)}) %collective-permute-start) | collective-permute-done | bytes 2097184 | tf_op jit(solution)/shard_map/while/body/eval_jaxpr/ppermute | solution.py:25
  1101.6 11.2 fusion.87
  1117.4 4.0 fusion.86
  1121.4 5.8 collective-permute-start
  1128.4 36.8 %collective-permute-done = f32[8,4,1,128,128]{4,3,2,1,0:T(8,128)} collective-permute-done((f32[8,4,1,128,128]{4,3,2,1,0:T(8,128)}, f32[8,4,1,128,128]{4,3,2,1,0:T(8,128)}, u32[]{:S(2)}, u32[]{:S(2)}) %collective-permute-start) | collective-permute-done | bytes 2097184 | tf_op jit(solution)/shard_map/while/body/eval_jaxpr/ppermute | solution.py:25
  1165.2 46.7 %collective-permute-done.1 = f32[8,4,1,128,128]{4,3,2,1,0:T(8,128)} collective-permute-done((f32[8,4,1,128,128]{4,3,2,1,0:T(8,128)S(1)}, f32[8,4,1,128,128]{4,3,2,1,0:T(8,128)}, u32[]{:S(2)}, u32[]{:S(2)}) %collective-permute-start.1) | collective-permute-done | bytes 2097184 | tf_op jit(solution)/shard_map/while/body/eval_jaxpr/ppermute | solution.py:27
  1211.9 11.2 fusion.87
  1231.7 5.9 collective-permute-start
  1238.9 41.6 %collective-permute-done = f32[8,4,1,128,128]{4,3,2,1,0:T(8,128)} collective-permute-done((f32[8,4,1,128,128]{4,3,2,1,0:T(8,128)}, f32[8,4,1,128,128]{4,3,2,1,0:T(8,128)}, u32[]{:S(2)}, u32[]{:S(2)}) %collective-permute-start) | collective-permute-done | bytes 2097184 | tf_op jit(solution)/shard_map/while/body/eval_jaxpr/ppermute | solution.py:25
  1280.5 46.8 %collective-permute-done.1 = f32[8,4,1,128,128]{4,3,2,1,0:T(8,128)} collective-permute-done((f32[8,4,1,128,128]{4,3,2,1,0:T(8,128)S(1)}, f32[8,4,1,128,128]{4,3,2,1,0:T(8,128)}, u32[]{:S(2)}, u32[]{:S(2)}) %collective-permute-start.1) | collective-permute-done | bytes 2097184 | tf_op jit(solution)/shard_map/while/body/eval_jaxpr/ppermute | solution.py:27
  1327.3 11.2 fusion.87
  1355.3 4.4 convolution_bitcast_fusion.1
  1359.7 4.4 convolution_bitcast_fusion
  1364.1 4.2 pad_maximum_fusion.3
  1368.4 113.7 %reduce-scatter.2.cloned.1.call-done = f32[8,2,2,128,128]{4,0,3,2,1:T(8,128)} async-done(((f32[32,2,2,128,128]{4,0,3,2,1:T(8,128)}), f32[8,2,2,128,128]{4,0,3,2,1:T(8,128)}) %reduce-scatter.2.cloned.1.call-update) | async-done | bytes 2097168 | tf_op jit(solution)/shard_map/reduce_scatter | solution.py:161
  (99 shorter events, 132.6 us)
Async XLA Ops:
  7.2 39.6 %all-gather.5.cloned.1.call-start = ((), (), s32[]{:S(2)}) async-start(), calls=%async_computation.2 | async-start | bytes 5242880 | tf_op jit(solution)/shard_map/all_gather | solution.py:138
  7.9 74.9 %all-gather.3.cloned.1.call-start = ((), (), s32[]{:S(2)}) async-start(), calls=%async_computation.1 | async-start | bytes 5242880 | tf_op jit(solution)/shard_map/all_gather | solution.py:137
  8.6 1473.4 %reduce-scatter.2.cloned.1.call-start = ((), (), s32[]{:S(2)}) async-start(), calls=%async_computation.3 | async-start | bytes 10485760 | tf_op jit(solution)/shard_map/reduce_scatter | solution.py:161
  87.4 2.2 copy-start
  120.8 93.9 %collective-permute-start = (f32[8,4,1,128,128]{4,3,2,1,0:T(8,128)}, f32[8,4,1,128,128]{4,3,2,1,0:T(8,128)}, u32[]{:S(2)}, u32[]{:S(2)}) collective-permute-start(f32[8,4,1,128,128]{4,3,2,1,0:T(8,128)} %get-tuple-element.332), channel_id=1, source_target_pairs={{0,1},{1,2},{2,3},{3,4},{4,5},{5,6},{6,7},{8,9},{9,10},{10,11},{11... | collective-permute-start | bytes 6291464 | tf_op jit(solution)/shard_map/while/body/eval_jaxpr/ppermute | solution.py:25
  125.5 89.1 %collective-permute-start.1 = (f32[8,4,1,128,128]{4,3,2,1,0:T(8,128)S(1)}, f32[8,4,1,128,128]{4,3,2,1,0:T(8,128)}, u32[]{:S(2)}, u32[]{:S(2)}) collective-permute-start(f32[8,4,1,128,128]{4,3,2,1,0:T(8,128)S(1)} %get-tuple-element.333), channel_id=1, source_target_pairs={{1,0},{2,1},{3,2},{4,3},{5,4},{6,5},{7,6},{9,8},{10,9},{11,10},{12... | collective-permute-start | bytes 6291464 | tf_op jit(solution)/shard_map/while/body/eval_jaxpr/ppermute | solution.py:27
  234.5 94.1 %collective-permute-start = (f32[8,4,1,128,128]{4,3,2,1,0:T(8,128)}, f32[8,4,1,128,128]{4,3,2,1,0:T(8,128)}, u32[]{:S(2)}, u32[]{:S(2)}) collective-permute-start(f32[8,4,1,128,128]{4,3,2,1,0:T(8,128)} %get-tuple-element.332), channel_id=1, source_target_pairs={{0,1},{1,2},{2,3},{3,4},{4,5},{5,6},{6,7},{8,9},{9,10},{10,11},{11... | collective-permute-start | bytes 6291464 | tf_op jit(solution)/shard_map/while/body/eval_jaxpr/ppermute | solution.py:25
  240.2 88.3 %collective-permute-start.1 = (f32[8,4,1,128,128]{4,3,2,1,0:T(8,128)S(1)}, f32[8,4,1,128,128]{4,3,2,1,0:T(8,128)}, u32[]{:S(2)}, u32[]{:S(2)}) collective-permute-start(f32[8,4,1,128,128]{4,3,2,1,0:T(8,128)S(1)} %get-tuple-element.333), channel_id=1, source_target_pairs={{1,0},{2,1},{3,2},{4,3},{5,4},{6,5},{7,6},{9,8},{10,9},{11,10},{12... | collective-permute-start | bytes 6291464 | tf_op jit(solution)/shard_map/while/body/eval_jaxpr/ppermute | solution.py:27
  348.3 93.2 %collective-permute-start = (f32[8,4,1,128,128]{4,3,2,1,0:T(8,128)}, f32[8,4,1,128,128]{4,3,2,1,0:T(8,128)}, u32[]{:S(2)}, u32[]{:S(2)}) collective-permute-start(f32[8,4,1,128,128]{4,3,2,1,0:T(8,128)} %get-tuple-element.332), channel_id=1, source_target_pairs={{0,1},{1,2},{2,3},{3,4},{4,5},{5,6},{6,7},{8,9},{9,10},{10,11},{11... | collective-permute-start | bytes 6291464 | tf_op jit(solution)/shard_map/while/body/eval_jaxpr/ppermute | solution.py:25
  354.1 87.4 %collective-permute-start.1 = (f32[8,4,1,128,128]{4,3,2,1,0:T(8,128)S(1)}, f32[8,4,1,128,128]{4,3,2,1,0:T(8,128)}, u32[]{:S(2)}, u32[]{:S(2)}) collective-permute-start(f32[8,4,1,128,128]{4,3,2,1,0:T(8,128)S(1)} %get-tuple-element.333), channel_id=1, source_target_pairs={{1,0},{2,1},{3,2},{4,3},{5,4},{6,5},{7,6},{9,8},{10,9},{11,10},{12... | collective-permute-start | bytes 6291464 | tf_op jit(solution)/shard_map/while/body/eval_jaxpr/ppermute | solution.py:27
  461.3 92.3 %collective-permute-start = (f32[8,4,1,128,128]{4,3,2,1,0:T(8,128)}, f32[8,4,1,128,128]{4,3,2,1,0:T(8,128)}, u32[]{:S(2)}, u32[]{:S(2)}) collective-permute-start(f32[8,4,1,128,128]{4,3,2,1,0:T(8,128)} %get-tuple-element.332), channel_id=1, source_target_pairs={{0,1},{1,2},{2,3},{3,4},{4,5},{5,6},{6,7},{8,9},{9,10},{10,11},{11... | collective-permute-start | bytes 6291464 | tf_op jit(solution)/shard_map/while/body/eval_jaxpr/ppermute | solution.py:25
  467.1 86.6 %collective-permute-start.1 = (f32[8,4,1,128,128]{4,3,2,1,0:T(8,128)S(1)}, f32[8,4,1,128,128]{4,3,2,1,0:T(8,128)}, u32[]{:S(2)}, u32[]{:S(2)}) collective-permute-start(f32[8,4,1,128,128]{4,3,2,1,0:T(8,128)S(1)} %get-tuple-element.333), channel_id=1, source_target_pairs={{1,0},{2,1},{3,2},{4,3},{5,4},{6,5},{7,6},{9,8},{10,9},{11,10},{12... | collective-permute-start | bytes 6291464 | tf_op jit(solution)/shard_map/while/body/eval_jaxpr/ppermute | solution.py:27
  573.5 91.5 %collective-permute-start = (f32[8,4,1,128,128]{4,3,2,1,0:T(8,128)}, f32[8,4,1,128,128]{4,3,2,1,0:T(8,128)}, u32[]{:S(2)}, u32[]{:S(2)}) collective-permute-start(f32[8,4,1,128,128]{4,3,2,1,0:T(8,128)} %get-tuple-element.332), channel_id=1, source_target_pairs={{0,1},{1,2},{2,3},{3,4},{4,5},{5,6},{6,7},{8,9},{9,10},{10,11},{11... | collective-permute-start | bytes 6291464 | tf_op jit(solution)/shard_map/while/body/eval_jaxpr/ppermute | solution.py:25
  579.2 85.7 %collective-permute-start.1 = (f32[8,4,1,128,128]{4,3,2,1,0:T(8,128)S(1)}, f32[8,4,1,128,128]{4,3,2,1,0:T(8,128)}, u32[]{:S(2)}, u32[]{:S(2)}) collective-permute-start(f32[8,4,1,128,128]{4,3,2,1,0:T(8,128)S(1)} %get-tuple-element.333), channel_id=1, source_target_pairs={{1,0},{2,1},{3,2},{4,3},{5,4},{6,5},{7,6},{9,8},{10,9},{11,10},{12... | collective-permute-start | bytes 6291464 | tf_op jit(solution)/shard_map/while/body/eval_jaxpr/ppermute | solution.py:27
  684.8 90.6 %collective-permute-start = (f32[8,4,1,128,128]{4,3,2,1,0:T(8,128)}, f32[8,4,1,128,128]{4,3,2,1,0:T(8,128)}, u32[]{:S(2)}, u32[]{:S(2)}) collective-permute-start(f32[8,4,1,128,128]{4,3,2,1,0:T(8,128)} %get-tuple-element.332), channel_id=1, source_target_pairs={{0,1},{1,2},{2,3},{3,4},{4,5},{5,6},{6,7},{8,9},{9,10},{10,11},{11... | collective-permute-start | bytes 6291464 | tf_op jit(solution)/shard_map/while/body/eval_jaxpr/ppermute | solution.py:25
  690.5 84.9 %collective-permute-start.1 = (f32[8,4,1,128,128]{4,3,2,1,0:T(8,128)S(1)}, f32[8,4,1,128,128]{4,3,2,1,0:T(8,128)}, u32[]{:S(2)}, u32[]{:S(2)}) collective-permute-start(f32[8,4,1,128,128]{4,3,2,1,0:T(8,128)S(1)} %get-tuple-element.333), channel_id=1, source_target_pairs={{1,0},{2,1},{3,2},{4,3},{5,4},{6,5},{7,6},{9,8},{10,9},{11,10},{12... | collective-permute-start | bytes 6291464 | tf_op jit(solution)/shard_map/while/body/eval_jaxpr/ppermute | solution.py:27
  795.2 89.8 %collective-permute-start = (f32[8,4,1,128,128]{4,3,2,1,0:T(8,128)}, f32[8,4,1,128,128]{4,3,2,1,0:T(8,128)}, u32[]{:S(2)}, u32[]{:S(2)}) collective-permute-start(f32[8,4,1,128,128]{4,3,2,1,0:T(8,128)} %get-tuple-element.332), channel_id=1, source_target_pairs={{0,1},{1,2},{2,3},{3,4},{4,5},{5,6},{6,7},{8,9},{9,10},{10,11},{11... | collective-permute-start | bytes 6291464 | tf_op jit(solution)/shard_map/while/body/eval_jaxpr/ppermute | solution.py:25
  801.0 84.0 %collective-permute-start.1 = (f32[8,4,1,128,128]{4,3,2,1,0:T(8,128)S(1)}, f32[8,4,1,128,128]{4,3,2,1,0:T(8,128)}, u32[]{:S(2)}, u32[]{:S(2)}) collective-permute-start(f32[8,4,1,128,128]{4,3,2,1,0:T(8,128)S(1)} %get-tuple-element.333), channel_id=1, source_target_pairs={{1,0},{2,1},{3,2},{4,3},{5,4},{6,5},{7,6},{9,8},{10,9},{11,10},{12... | collective-permute-start | bytes 6291464 | tf_op jit(solution)/shard_map/while/body/eval_jaxpr/ppermute | solution.py:27
  904.8 88.9 %collective-permute-start = (f32[8,4,1,128,128]{4,3,2,1,0:T(8,128)}, f32[8,4,1,128,128]{4,3,2,1,0:T(8,128)}, u32[]{:S(2)}, u32[]{:S(2)}) collective-permute-start(f32[8,4,1,128,128]{4,3,2,1,0:T(8,128)} %get-tuple-element.332), channel_id=1, source_target_pairs={{0,1},{1,2},{2,3},{3,4},{4,5},{5,6},{6,7},{8,9},{9,10},{10,11},{11... | collective-permute-start | bytes 6291464 | tf_op jit(solution)/shard_map/while/body/eval_jaxpr/ppermute | solution.py:25
  910.6 83.1 %collective-permute-start.1 = (f32[8,4,1,128,128]{4,3,2,1,0:T(8,128)S(1)}, f32[8,4,1,128,128]{4,3,2,1,0:T(8,128)}, u32[]{:S(2)}, u32[]{:S(2)}) collective-permute-start(f32[8,4,1,128,128]{4,3,2,1,0:T(8,128)S(1)} %get-tuple-element.333), channel_id=1, source_target_pairs={{1,0},{2,1},{3,2},{4,3},{5,4},{6,5},{7,6},{9,8},{10,9},{11,10},{12... | collective-permute-start | bytes 6291464 | tf_op jit(solution)/shard_map/while/body/eval_jaxpr/ppermute | solution.py:27
  1013.5 88.1 %collective-permute-start = (f32[8,4,1,128,128]{4,3,2,1,0:T(8,128)}, f32[8,4,1,128,128]{4,3,2,1,0:T(8,128)}, u32[]{:S(2)}, u32[]{:S(2)}) collective-permute-start(f32[8,4,1,128,128]{4,3,2,1,0:T(8,128)} %get-tuple-element.332), channel_id=1, source_target_pairs={{0,1},{1,2},{2,3},{3,4},{4,5},{5,6},{6,7},{8,9},{9,10},{10,11},{11... | collective-permute-start | bytes 6291464 | tf_op jit(solution)/shard_map/while/body/eval_jaxpr/ppermute | solution.py:25
  1019.3 82.3 %collective-permute-start.1 = (f32[8,4,1,128,128]{4,3,2,1,0:T(8,128)S(1)}, f32[8,4,1,128,128]{4,3,2,1,0:T(8,128)}, u32[]{:S(2)}, u32[]{:S(2)}) collective-permute-start(f32[8,4,1,128,128]{4,3,2,1,0:T(8,128)S(1)} %get-tuple-element.333), channel_id=1, source_target_pairs={{1,0},{2,1},{3,2},{4,3},{5,4},{6,5},{7,6},{9,8},{10,9},{11,10},{12... | collective-permute-start | bytes 6291464 | tf_op jit(solution)/shard_map/while/body/eval_jaxpr/ppermute | solution.py:27
  1121.4 43.8 %collective-permute-start = (f32[8,4,1,128,128]{4,3,2,1,0:T(8,128)}, f32[8,4,1,128,128]{4,3,2,1,0:T(8,128)}, u32[]{:S(2)}, u32[]{:S(2)}) collective-permute-start(f32[8,4,1,128,128]{4,3,2,1,0:T(8,128)} %get-tuple-element.332), channel_id=1, source_target_pairs={{0,1},{1,2},{2,3},{3,4},{4,5},{5,6},{6,7},{8,9},{9,10},{10,11},{11... | collective-permute-start | bytes 6291464 | tf_op jit(solution)/shard_map/while/body/eval_jaxpr/ppermute | solution.py:25
  1127.1 84.8 %collective-permute-start.1 = (f32[8,4,1,128,128]{4,3,2,1,0:T(8,128)S(1)}, f32[8,4,1,128,128]{4,3,2,1,0:T(8,128)}, u32[]{:S(2)}, u32[]{:S(2)}) collective-permute-start(f32[8,4,1,128,128]{4,3,2,1,0:T(8,128)S(1)} %get-tuple-element.333), channel_id=1, source_target_pairs={{1,0},{2,1},{3,2},{4,3},{5,4},{6,5},{7,6},{9,8},{10,9},{11,10},{12... | collective-permute-start | bytes 6291464 | tf_op jit(solution)/shard_map/while/body/eval_jaxpr/ppermute | solution.py:27
  1231.7 48.8 %collective-permute-start = (f32[8,4,1,128,128]{4,3,2,1,0:T(8,128)}, f32[8,4,1,128,128]{4,3,2,1,0:T(8,128)}, u32[]{:S(2)}, u32[]{:S(2)}) collective-permute-start(f32[8,4,1,128,128]{4,3,2,1,0:T(8,128)} %get-tuple-element.332), channel_id=1, source_target_pairs={{0,1},{1,2},{2,3},{3,4},{4,5},{5,6},{6,7},{8,9},{9,10},{10,11},{11... | collective-permute-start | bytes 6291464 | tf_op jit(solution)/shard_map/while/body/eval_jaxpr/ppermute | solution.py:25
  1237.6 89.7 %collective-permute-start.1 = (f32[8,4,1,128,128]{4,3,2,1,0:T(8,128)S(1)}, f32[8,4,1,128,128]{4,3,2,1,0:T(8,128)}, u32[]{:S(2)}, u32[]{:S(2)}) collective-permute-start(f32[8,4,1,128,128]{4,3,2,1,0:T(8,128)S(1)} %get-tuple-element.333), channel_id=1, source_target_pairs={{1,0},{2,1},{3,2},{4,3},{5,4},{6,5},{7,6},{9,8},{10,9},{11,10},{12... | collective-permute-start | bytes 6291464 | tf_op jit(solution)/shard_map/while/body/eval_jaxpr/ppermute | solution.py:27
Sparse Core Ops, SparseCore 0:
  9.5 37.1 all-gather.4
  48.3 34.4 all-gather.2
  1368.5 113.5 reduce-scatter.1
where the time goes:
time: 1500 us; the launch traced here: 1490 us
  waiting for transfers between devices  1110 us (74%)
  other arithmetic  182 us (12%)
  local copies, waits for them, and re-layouts  79.2 us (5%)
  starting transfers between devices  76.9 us (5%)
  matrix products  27.6 us (2%)
    ppermute x11, waiting for transfers between devices, padded_2(): lax.ppermute(tail, axis, [(i, (i + 1) % count) for i in range(ends)])  838 us
    add x11, other arithmetic, sweep(): return block_solve(coefficient, sources + MU * neighbour_sum(zpadded))  123 us
    reduce_scatter x1, waiting for transfers between devices, body(): lax.psum_scatter(jnp.stack((state_time, adjoint_time), axis=1), 'tm', sca...  114 us
    ppermute x11, waiting for transfers between devices, padded_2(): lax.ppermute(head, axis, [((i + 1) % count, i) for i in range(ends)])  93.6 us
    ppermute x11, starting transfers between devices, padded_2(): lax.ppermute(tail, axis, [(i, (i + 1) % count) for i in range(ends)])  62.7 us
    slice x11, local copies, waits for them, and re-layouts, padded_2(): head = lax.slice_in_dim(cells, 0, width, axis=dim)  43.5 us
    all_gather x1, waiting for transfers between devices, body(): lax.all_gather(adjoint_rhs, 'tm', axis=0, tiled=True)  36.7 us
  transfers between devices with their start and end apart: 25, of which 16 were waited for; matrix products, arithmetic and copies ran while one was open for 1% of the time, Pallas kernels for 0%

commit v1 on v0

--- a/solution.py
+++ b/solution.py
@@ -1,8 +1,12 @@
+import functools
 import math
 
 import jax
 import jax.numpy as jnp
+import numpy as np
 from jax import lax
+from jax.experimental import pallas as pl
+from jax.experimental.pallas import tpu as pltpu
 from jax.sharding import PartitionSpec as P
 
 STEPS = 32
@@ -166,7 +170,349 @@
     return (state_out, adjoint_out)
 
 
+MESH = pl.DeviceIdType.MESH
+
+
+def cmul_const(factor, value):
+    re, im = value
+    a, b = float(factor.real), float(factor.imag)
+    if abs(b) < 1e-12 and abs(a - 1.0) < 1e-12:
+        return value
+    if abs(a) < 1e-12:
+        return (-im, re) if b > 0 else (im, -re)
+    if abs(abs(a) - abs(b)) < 1e-12:
+        sa, sb = math.copysign(1.0, a), math.copysign(1.0, b)
+        first = re - im if sa * sb > 0 else re + im
+        second = im + re if sa * sb > 0 else im - re
+        return first * (sa * abs(a)), second * (sa * abs(a))
+    return a * re - b * im, a * im + b * re
+
+
+def fft_list(load, indices, sign):
+    count = len(indices)
+    if count == 1:
+        return [load(indices[0])]
+    even = fft_list(load, indices[0::2], sign)
+    odd = fft_list(load, indices[1::2], sign)
+    half = count // 2
+    low, high = [], []
+    for k in range(half):
+        t = cmul_const(np.exp(sign * 2j * math.pi * k / count), odd[k])
+        low.append((even[k][0] + t[0], even[k][1] + t[1]))
+        high.append((even[k][0] - t[0], even[k][1] - t[1]))
+    return low + high
+
+
+PAD = 8
+
+
+def whole_kernel(
+    dims, lam_ref, s_ref, a_ref, re_ref, so_ref, ao_ref,
+    r1, hat, src, full, coef, u0, u1, back, outs,
+    s_a, r_a, s_b, r_b, s_d, r_d, s_f, r_f, s_r, r_r, s_q, r_q, loc,
+):
+    groups, slabs, local, depth, nx, ny = dims
+    steps = groups * local
+    devices = groups * slabs
+    nz = depth * slabs
+    xb = nx // groups
+    rows = xb // 2
+    chunks = depth * 2
+    t, s = lax.axis_index("tm"), lax.axis_index("space")
+    me = t * slabs + s
+    half_x = nx // 2
+    part = lax.rem(t, 2)
+    partner = t + 1 - 2 * part
+
+    def at_chunk(ch):
+        return ch // 2, pl.multiple_of(lax.rem(ch, 2) * rows, rows)
+
+    def xrow(block, row, base=0):
+        return pl.ds(pl.multiple_of(base + block * xb + row, 8), rows)
+
+    def half():
+        return pl.ds(pl.multiple_of(part * half_x, 8), half_x)
+
+    def reaction_send(j):
+        s2 = lax.rem(s + j, slabs)
+        return pltpu.make_async_remote_copy(
+            re_ref.at[:, half(), :], full.at[pl.ds(s * depth, depth), half(), :],
+            s_r, r_r, device_id=(t, s2), device_id_type=MESH)
+
+    lax.fori_loop(1, slabs, lambda j, c: (reaction_send(j).start(), c)[1], 0)
+    own_reaction = pltpu.make_async_copy(
+        re_ref.at[:, half(), :], full.at[pl.ds(s * depth, depth), half(), :], loc.at[0])
+    own_reaction.start()
+
+    def a_copy(arr, ch, j):
+        z, row = at_chunk(ch)
+        t2 = lax.rem(t + j, groups)
+        ref = s_ref if arr == 0 else a_ref
+        return pltpu.make_async_remote_copy(
+            ref.at[:, z, xrow(t2, row), :],
+            r1.at[arr, pl.ds(t * local, local), z, pl.ds(row, rows), :],
+            s_a.at[ch, arr, j - 1], r_a.at[ch, arr, j - 1],
+            device_id=(t2, s), device_id_type=MESH)
+
+    def start_a(ch, c):
+        for j in range(1, groups):
+            for arr in range(2):
+                a_copy(arr, ch, j).start()
+        return c
+
+    lax.fori_loop(0, chunks, start_a, 0)
+    mine = pl.ds(pl.multiple_of(t * xb, 8), xb)
+    own_a = [
+        pltpu.make_async_copy(
+            ref.at[:, :, mine, :], r1.at[arr, pl.ds(t * local, local)], loc.at[1 + arr])
+        for arr, ref in enumerate((s_ref, a_ref))
+    ]
+    for c in own_a:
+        c.start()
+
+    zero = jnp.zeros((nx + 2 * PAD, ny), jnp.float32)
+    for buf in (u0, u1):
+        def clear(z, c, buf=buf):
+            for comp in range(2):
+                buf[comp, z] = zero
+            return c
+        lax.fori_loop(0, nz + 2, clear, 0)
+    for c in own_a:
+        c.wait()
+
+    growth = [math.exp(math.log(ALPHA) * n / steps) for n in range(steps)]
+
+    def b_copy(ch, j):
+        z, row = at_chunk(ch)
+        d = lax.rem(me + j, devices)
+        return pltpu.make_async_remote_copy(
+            hat.at[d, :, z, pl.ds(row, rows), :],
+            src.at[:, s * depth + z, xrow(t, row), :],
+            s_b, r_b, device_id=(d // slabs, lax.rem(d, slabs)), device_id_type=MESH)
+
+    def forward(ch, c):
+        z, row = at_chunk(ch)
+        for j in range(1, groups):
+            for arr in range(2):
+                a_copy(arr, ch, j).wait_recv()
+
+        def piece(r, c):
+            at = pl.ds(pl.multiple_of(row + r * 8, 8), 8)
+
+            def load(n):
+                return r1[0, n, z, at, :] * growth[n], r1[1, steps - 1 - n, z, at, :] * growth[n]
+
+            for k, (re, im) in enumerate(fft_list(load, list(range(steps)), -1)):
+                hat[k, 0, z, at, :] = re
+                hat[k, 1, z, at, :] = im
+            return c
+
+        lax.fori_loop(0, rows // 8, piece, 0)
+        lax.fori_loop(1, devices, lambda j, c: (b_copy(ch, j).start(), c)[1], 0)
+        return c
+
+    lax.fori_loop(0, chunks, forward, 0)
+    own_b = pltpu.make_async_copy(
+        hat.at[me], src.at[:, pl.ds(s * depth, depth), mine, :], loc.at[3])
+    own_b.start()
+
+    many = full.at[pl.ds(0, (slabs - 1) * depth), pl.ds(0, half_x), :]
+    pltpu.make_async_copy(many, many, r_r).wait()
+    own_reaction.wait()
+    swap = pltpu.make_async_remote_copy(
+        full.at[:, half(), :], full.at[:, half(), :], s_q, r_q,
+        device_id=(partner, s), device_id_type=MESH)
+    swap.start()
+    swap.wait()
+    l_re = lam_ref[me, 0] + MU * 6.0
+    l_im = lam_ref[me, 1] + BETA
+
+    def coefs(z, c):
+        e_re = MU * full[z] + l_re
+        inv = 1.0 / (e_re * e_re + l_im * l_im)
+        coef[0, z] = e_re * inv
+        coef[1, z] = -l_im * inv
+        return c
+
+    lax.fori_loop(0, nz, coefs, 0)
+    own_b.wait()
+    most = hat.at[pl.ds(0, devices - 1)]
+    pltpu.make_async_copy(most, most, r_b).wait()
+
+    xc = 32
+    lane = lax.broadcasted_iota(jnp.int32, (xc, ny), 1)
+
+    def sweep(cur, new):
+        def plane(z, c):
+            for x0 in range(0, nx, xc):
+                sums = []
+                for comp in range(2):
+                    total = src[comp, z, x0:x0 + xc, :]
+                    if cur is not None:
+                        mid = cur[comp, z + 1, PAD + x0:PAD + x0 + xc, :]
+                        nb = cur[comp, z + 2, PAD + x0:PAD + x0 + xc, :]
+                        nb = nb + cur[comp, z, PAD + x0:PAD + x0 + xc, :]
+                        nb = nb + cur[comp, z + 1, PAD + x0 + 1:PAD + x0 + 1 + xc, :]
+                        nb = nb + cur[comp, z + 1, PAD + x0 - 1:PAD + x0 - 1 + xc, :]
+                        nb = nb + jnp.where(lane == 0, 0.0, pltpu.roll(mid, 1, 1))
+                        nb = nb + jnp.where(lane == ny - 1, 0.0, pltpu.roll(mid, ny - 1, 1))
+                        total = total + MU * nb
+                    sums.append(total)
+                c_re = coef[0, z, x0:x0 + xc, :]
+                c_im = coef[1, z, x0:x0 + xc, :]
+                new[0, z + 1, PAD + x0:PAD + x0 + xc, :] = c_re * sums[0] - c_im * sums[1]
+                new[1, z + 1, PAD + x0:PAD + x0 + xc, :] = c_re * sums[1] + c_im * sums[0]
+            return c
+
+        lax.fori_loop(0, nz, plane, 0)
+
+    sweep(None, u0)
+
+    def two(i, c):
+        sweep(u0, u1)
+        sweep(u1, u0)
+        return c
+
+    lax.fori_loop(0, (SWEEPS - 1) // 2, two, 0)
+    last = u0
+    if (SWEEPS - 1) % 2:
+        sweep(u0, u1)
+        last = u1
+
+    def d_copy(ch, j):
+        z, row = at_chunk(ch)
+        d = lax.rem(me + j, devices)
+        t2, s2 = d // slabs, lax.rem(d, slabs)
+        return pltpu.make_async_remote_copy(
+            last.at[:, 1 + s2 * depth + z, xrow(t2, row, PAD), :],
+            back.at[me, :, z, pl.ds(row, rows), :],
+            s_d, r_d.at[ch], device_id=(t2, s2), device_id_type=MESH)
+
+    def start_d(ch, c):
+        lax.fori_loop(1, devices, lambda j, c: (d_copy(ch, j).start(), c)[1], 0)
+        return c
+
+    lax.fori_loop(0, chunks, start_d, 0)
+    own_d = pltpu.make_async_copy(
+        last.at[:, pl.ds(1 + s * depth, depth), pl.ds(pl.multiple_of(PAD + t * xb, 8), xb), :],
+        back.at[me], loc.at[4])
+    own_d.start()
+    own_d.wait()
+    shrink = [math.exp(-math.log(ALPHA) * n / steps) / steps for n in range(steps)]
+
+    def f_copy(arr, ch, j):
+        z, row = at_chunk(ch)
+        t2 = lax.rem(t + j, groups)
+        ref = so_ref if arr == 0 else ao_ref
+        return pltpu.make_async_remote_copy(
+            outs.at[arr, pl.ds(t2 * local, local), z, pl.ds(row, rows), :],
+            ref.at[:, z, xrow(t, row), :],
+            s_f.at[ch, arr, j - 1], r_f.at[ch, arr, j - 1],
+            device_id=(t2, s), device_id_type=MESH)
+
+    def backward(ch, c):
+        z, row = at_chunk(ch)
+        got = back.at[pl.ds(0, devices - 1), :, z, pl.ds(row, rows), :]
+        pltpu.make_async_copy(got, got, r_d.at[ch]).wait()
+
+        def piece(r, c):
+            at = pl.ds(pl.multiple_of(row + r * 8, 8), 8)
+
+            def load(k):
+                return back[k, 0, z, at, :], back[k, 1, z, at, :]
+
+            for n, (re, im) in enumerate(fft_list(load, list(range(steps)), 1)):
+                outs[0, n, z, at, :] = re * shrink[n]
+                outs[1, steps - 1 - n, z, at, :] = im * shrink[n]
+            return c
+
+        lax.fori_loop(0, rows // 8, piece, 0)
+        for j in range(1, groups):
+            for arr in range(2):
+                f_copy(arr, ch, j).start()
+        return c
+
+    lax.fori_loop(0, chunks, backward, 0)
+    own_f = [
+        pltpu.make_async_copy(
+            outs.at[arr, pl.ds(t * local, local)], ref.at[:, :, mine, :], loc.at[5 + arr])
+        for arr, ref in enumerate((so_ref, ao_ref))
+    ]
+    for c in own_f:
+        c.start()
+    for c in own_f:
+        c.wait()
+
+    def finish(ch, c):
+        for j in range(1, groups):
+            for arr in range(2):
+                a_copy(arr, ch, j).wait_send()
+                f_copy(arr, ch, j).wait()
+        return c
+
+    lax.fori_loop(0, chunks, finish, 0)
+    pltpu.make_async_copy(most, most, s_b).wait()
+    pltpu.make_async_copy(most, most, s_d).wait()
+    pltpu.make_async_copy(many, many, s_r).wait()
+
+
+def fused_body(state_rhs, adjoint_rhs, reaction):
+    groups, slabs = lax.axis_size("tm"), lax.axis_size("space")
+    local, depth, nx, ny = state_rhs.shape
+    dims = (groups, slabs, local, depth, nx, ny)
+    steps, devices, nz, xb = groups * local, groups * slabs, depth * slabs, nx // groups
+    chunks = depth * 2
+    turn = 2.0 * math.pi * np.arange(steps) / steps
+    rate = ALPHA ** (1.0 / steps)
+    lam = np.stack((1.0 - rate * np.cos(turn), rate * np.sin(turn)), axis=1).astype(np.float32)
+    f32 = jnp.float32
+    dma = pltpu.SemaphoreType.DMA
+    vmem = pl.BlockSpec(memory_space=pltpu.VMEM)
+    shape = jax.ShapeDtypeStruct(state_rhs.shape, f32)
+    return pl.pallas_call(
+        functools.partial(whole_kernel, dims),
+        out_shape=(shape, shape),
+        in_specs=[pl.BlockSpec(memory_space=pltpu.SMEM), vmem, vmem, vmem],
+        out_specs=(vmem, vmem),
+        scratch_shapes=[
+            pltpu.VMEM((2, steps, depth, xb, ny), f32),
+            pltpu.VMEM((devices, 2, depth, xb, ny), f32),
+            pltpu.VMEM((2, nz, nx, ny), f32),
+            pltpu.VMEM((nz, nx, ny), f32),
+            pltpu.VMEM((2, nz, nx, ny), f32),
+            pltpu.VMEM((2, nz + 2, nx + 2 * PAD, ny), f32),
+            pltpu.VMEM((2, nz + 2, nx + 2 * PAD, ny), f32),
+            pltpu.VMEM((devices, 2, depth, xb, ny), f32),
+            pltpu.VMEM((2, steps, depth, xb, ny), f32),
+            dma((chunks, 2, groups - 1)),
+            dma((chunks, 2, groups - 1)),
+            dma,
+            dma,
+            dma,
+            dma((chunks,)),
+            dma((chunks, 2, groups - 1)),
+            dma((chunks, 2, groups - 1)),
+            dma,
+            dma,
+            dma,
+            dma,
+            dma((7,)),
+        ],
+        compiler_params=pltpu.CompilerParams(
+            has_side_effects=True, vmem_limit_bytes=58 * 1024 * 1024
+        ),
+    )(jnp.asarray(lam), state_rhs, adjoint_rhs, reaction)
+
+
 def solution(mesh):
     in_specs = (P("tm", "space", None, None), P("tm", "space", None, None), P("space", None, None))
     out_specs = (P("tm", "space", None, None), P("tm", "space", None, None))
-    return jax.shard_map(body, mesh=mesh, in_specs=in_specs, out_specs=out_specs, check_vma=False)
+    groups, slabs = mesh.shape["tm"], mesh.shape["space"]
+
+    def chosen(state_rhs, adjoint_rhs, reaction):
+        steps = state_rhs.shape[0] * groups
+        fits = steps == groups * slabs and steps & (steps - 1) == 0 and groups % 2 == 0
+        fits = fits and state_rhs.shape[2] % (16 * groups) == 0 and state_rhs.shape[3] == 128
+        return (fused_body if fits else body)(state_rhs, adjoint_rhs, reaction)
+
+    return jax.shard_map(chosen, mesh=mesh, in_specs=in_specs, out_specs=out_specs, check_vma=False)

time: 1500 us -> 155 us (0.10)
  waiting for transfers between devices: 1110 us -> 0 us
  other arithmetic: 182 us -> 0 us
  Pallas kernels: 0 us -> 150 us
  starting transfers between devices: 76.9 us -> 0 us
  local copies, waits for them, and re-layouts: 79.2 us -> 3.36 us
  matrix products: 27.6 us -> 0 us
    ppermute x22 -> x0, waiting for transfers between devices: 932 us -> none  [the longest x11 838 us: padded_2(): lax.ppermute(tail, axis, [(i, (i + 1) % count) for i in range(ends)])]
    pallas_call x0 -> x1, Pallas kernels: none -> 150 us  [fused_body(): pl.pallas_call(functools.partial(whole_kernel, dims), out_shape=(shape, s...]
    add x26 -> x0, other arithmetic: 142 us -> none  [the longest x11 123 us: sweep(): return block_solve(coefficient, sources + MU * neighbour_sum(zpadded))]
    reduce_scatter x1 -> x0, waiting for transfers between devices: 114 us -> none  [body(): lax.psum_scatter(jnp.stack((state_time, adjoint_time), axis=1), 'tm', sca...]
    ppermute x22 -> x0, starting transfers between devices: 76.8 us -> none  [the longest x11 62.7 us: padded_2(): lax.ppermute(tail, axis, [(i, (i + 1) % count) for i in range(ends)])]
    all_gather x2 -> x0, waiting for transfers between devices: 65.3 us -> none  [the longest x1 36.7 us: body(): lax.all_gather(adjoint_rhs, 'tm', axis=0, tiled=True)]
    slice x12 -> x0, local copies, waits for them, and re-layouts: 47.4 us -> none  [the longest x11 43.5 us: padded_2(): head = lax.slice_in_dim(cells, 0, width, axis=dim)]
    another operation x14 -> x0, other arithmetic: 29.4 us -> none  [the longest x12 25.2 us: block_solve(): return jnp.stack((new_yre, new_yim, new_pre, new_pim), axis=-4)]
  transfers between devices with their start and end apart: 25 -> 0, of which waited for: 16 -> 0; matrix products, arithmetic and copies ran while one was open for 1% -> 0% of each run, Pallas kernels for 0% -> 0%
where the time goes in v1:
time: 155 us; the launch traced here: 154 us
  Pallas kernels  150 us (97%)
  local copies, waits for them, and re-layouts  3.36 us (2%)
    pallas_call x1, Pallas kernels, fused_body(): pl.pallas_call(functools.partial(whole_kernel, dims), out_shape=(shape, s...  150 us
    unnamed x4, local copies, waits for them, and re-layouts  3.36 us

profile of v1, /device:TPU:0, one launch (start us, length us, event | category | flops | bytes accessed | tf_op | source)
XLA Modules:
  0.0 153.9 jit_solution(13374074283693801980)
XLA Ops:
  0.6 149.9 %shard_map.59 = (f32[8,2,128,128]{3,2,1,0:T(8,128)}, f32[8,2,128,128]{3,2,1,0:T(8,128)}) custom-call(f32[32,2]{1,0:T(8,128)} %constant.2.clone.lam_ref, f32[8,2,128,128]{3,2,1,0:T(8,128)} %s_ref.1, f32[8,2,128,128]{3,2,1,0:T(8,128)} %a_ref.1, f32[2,128,128]{2,1,0:T(8,128)} %re_ref.1), custom_call_target="tpu_custom_call" | custom-call | tf_op jit(solution)/shard_map/pallas_call | solution.py:472
  150.5 0.0 copy-start
  150.5 2.4 %copy.8 = f32[8,2,128,128]{3,2,1,0:T(8,128)} copy(f32[8,2,128,128]{3,2,1,0:T(8,128)} %get-tuple-element.4) | data formatting | bytes 2097152
  152.9 0.0 copy-done
  152.9 1.0 copy.9
Async XLA Ops:
  150.5 2.4 %copy-start = (f32[8,2,128,128]{3,2,1,0:T(8,128)S(1)}, f32[8,2,128,128]{3,2,1,0:T(8,128)}, u32[]{:S(2)}) copy-start(f32[8,2,128,128]{3,2,1,0:T(8,128)} %get-tuple-element.5) | copy-start | bytes 3145732

commit v2 on v1

--- a/solution.py
+++ b/solution.py
@@ -203,54 +203,68 @@
     return low + high
 
 
-PAD = 8
+LOW, HIGH = 16, 24
 
 
 def whole_kernel(
     dims, lam_ref, s_ref, a_ref, re_ref, so_ref, ao_ref,
     r1, hat, src, full, coef, u0, u1, back, outs,
-    s_a, r_a, s_b, r_b, s_d, r_d, s_f, r_f, s_r, r_r, s_q, r_q, loc,
+    s_a, r_a, s_b, r_b, s_d, r_d, s_f, r_f, s_r, r_r, s_y, r_y, s_q, r_q, loc,
 ):
     groups, slabs, local, depth, nx, ny = dims
     steps = groups * local
     devices = groups * slabs
     nz = depth * slabs
     xb = nx // groups
-    rows = xb // 2
-    chunks = depth * 2
+    rows = 8
+    chunks = xb // rows
+    xstep = nx // chunks
     t, s = lax.axis_index("tm"), lax.axis_index("space")
     me = t * slabs + s
     half_x = nx // 2
     part = lax.rem(t, 2)
     partner = t + 1 - 2 * part
 
-    def at_chunk(ch):
-        return ch // 2, pl.multiple_of(lax.rem(ch, 2) * rows, rows)
-
-    def xrow(block, row, base=0):
-        return pl.ds(pl.multiple_of(base + block * xb + row, 8), rows)
+    def kept(ch):
+        return pl.ds(pl.multiple_of(ch * rows, rows), rows)
+
+    def xrow(ch, member, base=0):
+        return pl.ds(pl.multiple_of(base + ch * xstep + member * rows, rows), rows)
 
     def half():
         return pl.ds(pl.multiple_of(part * half_x, 8), half_x)
 
     def reaction_send(j):
-        s2 = lax.rem(s + j, slabs)
+        s2 = lax.rem(s + 2 * j, slabs)
         return pltpu.make_async_remote_copy(
             re_ref.at[:, half(), :], full.at[pl.ds(s * depth, depth), half(), :],
             s_r, r_r, device_id=(t, s2), device_id_type=MESH)
 
-    lax.fori_loop(1, slabs, lambda j, c: (reaction_send(j).start(), c)[1], 0)
+    parity = lax.rem(s, 2)
+
+    def parity_send(i):
+        planes = full.at[pl.ds((2 * i + parity) * depth, depth), half(), :]
+        return pltpu.make_async_remote_copy(
+            planes, planes, s_y, r_y, device_id=(t, s + 1 - 2 * parity), device_id_type=MESH)
+
+    def planes_of(count):
+        return full.at[pl.ds(0, count * depth), pl.ds(0, half_x), :]
+
+    def wait_bytes(ref, sem):
+        pltpu.make_async_copy(ref, ref, sem).wait()
+
+    for j in range(1, slabs // 2):
+        reaction_send(j).start()
     own_reaction = pltpu.make_async_copy(
-        re_ref.at[:, half(), :], full.at[pl.ds(s * depth, depth), half(), :], loc.at[0])
+        re_ref.at[:, half(), :], full.at[pl.ds(s * depth, depth), half(), :], loc.at[0, 0, 0])
     own_reaction.start()
 
     def a_copy(arr, ch, j):
-        z, row = at_chunk(ch)
         t2 = lax.rem(t + j, groups)
         ref = s_ref if arr == 0 else a_ref
         return pltpu.make_async_remote_copy(
-            ref.at[:, z, xrow(t2, row), :],
-            r1.at[arr, pl.ds(t * local, local), z, pl.ds(row, rows), :],
+            ref.at[:, :, xrow(ch, t2), :],
+            r1.at[arr, pl.ds(t * local, local), :, kept(ch), :],
             s_a.at[ch, arr, j - 1], r_a.at[ch, arr, j - 1],
             device_id=(t2, s), device_id_type=MESH)
 
@@ -261,43 +275,56 @@
         return c
 
     lax.fori_loop(0, chunks, start_a, 0)
-    mine = pl.ds(pl.multiple_of(t * xb, 8), xb)
     own_a = [
         pltpu.make_async_copy(
-            ref.at[:, :, mine, :], r1.at[arr, pl.ds(t * local, local)], loc.at[1 + arr])
+            ref.at[:, :, xrow(ch, t), :],
+            r1.at[arr, pl.ds(t * local, local), :, kept(ch), :], loc.at[1, arr, ch])
         for arr, ref in enumerate((s_ref, a_ref))
+        for ch in range(chunks)
     ]
     for c in own_a:
         c.start()
 
-    zero = jnp.zeros((nx + 2 * PAD, ny), jnp.float32)
-    for buf in (u0, u1):
+    zero = jnp.zeros((LOW + nx + HIGH, ny), jnp.float32)
+    for buf, extra in ((u0, 2), (u1, 2)):
         def clear(z, c, buf=buf):
             for comp in range(2):
                 buf[comp, z] = zero
             return c
-        lax.fori_loop(0, nz + 2, clear, 0)
+        lax.fori_loop(0, nz + extra, clear, 0)
+
+    def clear_edges(z, c):
+        for buf in (src, coef):
+            for comp in range(2):
+                buf[comp, z, 0:LOW, :] = zero[0:LOW]
+                buf[comp, z, LOW + nx:, :] = zero[0:HIGH]
+        return c
+
+    lax.fori_loop(0, nz, clear_edges, 0)
     for c in own_a:
         c.wait()
 
     growth = [math.exp(math.log(ALPHA) * n / steps) for n in range(steps)]
 
     def b_copy(ch, j):
-        z, row = at_chunk(ch)
         d = lax.rem(me + j, devices)
         return pltpu.make_async_remote_copy(
-            hat.at[d, :, z, pl.ds(row, rows), :],
-            src.at[:, s * depth + z, xrow(t, row), :],
-            s_b, r_b, device_id=(d // slabs, lax.rem(d, slabs)), device_id_type=MESH)
+            hat.at[d, :, :, kept(ch), :],
+            src.at[:, pl.ds(s * depth, depth), xrow(ch, t, LOW), :],
+            s_b, r_b.at[ch], device_id=(d // slabs, lax.rem(d, slabs)), device_id_type=MESH)
+
+    def own_b(ch):
+        return pltpu.make_async_copy(
+            hat.at[me, :, :, kept(ch), :],
+            src.at[:, pl.ds(s * depth, depth), xrow(ch, t, LOW), :], loc.at[2, 0, ch])
 
     def forward(ch, c):
-        z, row = at_chunk(ch)
         for j in range(1, groups):
             for arr in range(2):
                 a_copy(arr, ch, j).wait_recv()
 
-        def piece(r, c):
-            at = pl.ds(pl.multiple_of(row + r * 8, 8), 8)
+        def piece(z, c):
+            at = kept(ch)
 
             def load(n):
                 return r1[0, n, z, at, :] * growth[n], r1[1, steps - 1 - n, z, at, :] * growth[n]
@@ -307,18 +334,19 @@
                 hat[k, 1, z, at, :] = im
             return c
 
-        lax.fori_loop(0, rows // 8, piece, 0)
+        lax.fori_loop(0, depth, piece, 0)
         lax.fori_loop(1, devices, lambda j, c: (b_copy(ch, j).start(), c)[1], 0)
+        own_b(ch).start()
         return c
 
-    lax.fori_loop(0, chunks, forward, 0)
-    own_b = pltpu.make_async_copy(
-        hat.at[me], src.at[:, pl.ds(s * depth, depth), mine, :], loc.at[3])
-    own_b.start()
-
-    many = full.at[pl.ds(0, (slabs - 1) * depth), pl.ds(0, half_x), :]
-    pltpu.make_async_copy(many, many, r_r).wait()
+    lax.fori_loop(0, 1, forward, 0)
+    wait_bytes(planes_of(slabs // 2 - 1), r_r)
     own_reaction.wait()
+    for i in range(slabs // 2):
+        parity_send(i).start()
+    lax.fori_loop(1, chunks, forward, 0)
+
+    wait_bytes(planes_of(slabs // 2), r_y)
     swap = pltpu.make_async_remote_copy(
         full.at[:, half(), :], full.at[:, half(), :], s_q, r_q,
         device_id=(partner, s), device_id_type=MESH)
@@ -330,93 +358,89 @@
     def coefs(z, c):
         e_re = MU * full[z] + l_re
         inv = 1.0 / (e_re * e_re + l_im * l_im)
-        coef[0, z] = e_re * inv
-        coef[1, z] = -l_im * inv
+        coef[0, z, LOW:LOW + nx, :] = e_re * inv
+        coef[1, z, LOW:LOW + nx, :] = -l_im * inv
         return c
 
     lax.fori_loop(0, nz, coefs, 0)
-    own_b.wait()
-    most = hat.at[pl.ds(0, devices - 1)]
-    pltpu.make_async_copy(most, most, r_b).wait()
-
-    xc = 32
-    lane = lax.broadcasted_iota(jnp.int32, (xc, ny), 1)
-
-    def sweep(cur, new):
-        def plane(z, c):
-            for x0 in range(0, nx, xc):
-                sums = []
-                for comp in range(2):
-                    total = src[comp, z, x0:x0 + xc, :]
-                    if cur is not None:
-                        mid = cur[comp, z + 1, PAD + x0:PAD + x0 + xc, :]
-                        nb = cur[comp, z + 2, PAD + x0:PAD + x0 + xc, :]
-                        nb = nb + cur[comp, z, PAD + x0:PAD + x0 + xc, :]
-                        nb = nb + cur[comp, z + 1, PAD + x0 + 1:PAD + x0 + 1 + xc, :]
-                        nb = nb + cur[comp, z + 1, PAD + x0 - 1:PAD + x0 - 1 + xc, :]
-                        nb = nb + jnp.where(lane == 0, 0.0, pltpu.roll(mid, 1, 1))
-                        nb = nb + jnp.where(lane == ny - 1, 0.0, pltpu.roll(mid, ny - 1, 1))
-                        total = total + MU * nb
-                    sums.append(total)
-                c_re = coef[0, z, x0:x0 + xc, :]
-                c_im = coef[1, z, x0:x0 + xc, :]
-                new[0, z + 1, PAD + x0:PAD + x0 + xc, :] = c_re * sums[0] - c_im * sums[1]
-                new[1, z + 1, PAD + x0:PAD + x0 + xc, :] = c_re * sums[1] + c_im * sums[0]
-            return c
-
-        lax.fori_loop(0, nz, plane, 0)
-
-    sweep(None, u0)
-
-    def two(i, c):
-        sweep(u0, u1)
-        sweep(u1, u0)
-        return c
-
-    lax.fori_loop(0, (SWEEPS - 1) // 2, two, 0)
-    last = u0
-    if (SWEEPS - 1) % 2:
-        sweep(u0, u1)
-        last = u1
+
+    def tile(c, j, width):
+        x0 = LOW + c * xstep - j
+        cur, new = (u0, u1) if j % 2 else (u1, u0)
+        lane = lax.broadcasted_iota(jnp.int32, (width, ny), 1)
+
+        def plane(z, carry):
+            sums = []
+            for comp in range(2):
+                total = src[comp, z, x0:x0 + width, :]
+                if j > 0:
+                    mid = cur[comp, z + 1, x0:x0 + width, :]
+                    nb = cur[comp, z + 2, x0:x0 + width, :]
+                    nb = nb + cur[comp, z, x0:x0 + width, :]
+                    nb = nb + cur[comp, z + 1, x0 + 1:x0 + 1 + width, :]
+                    nb = nb + cur[comp, z + 1, x0 - 1:x0 - 1 + width, :]
+                    nb = nb + jnp.where(lane == 0, 0.0, pltpu.roll(mid, 1, 1))
+                    nb = nb + jnp.where(lane == ny - 1, 0.0, pltpu.roll(mid, ny - 1, 1))
+                    total = total + MU * nb
+                sums.append(total)
+            c_re = coef[0, z, x0:x0 + width, :]
+            c_im = coef[1, z, x0:x0 + width, :]
+            new[0, z + 1, x0:x0 + width, :] = c_re * sums[0] - c_im * sums[1]
+            new[1, z + 1, x0:x0 + width, :] = c_re * sums[1] + c_im * sums[0]
+            return carry
+
+        lax.fori_loop(0, nz, plane, 0, unroll=2)
+
+    last = u0 if SWEEPS % 2 else u1
 
     def d_copy(ch, j):
-        z, row = at_chunk(ch)
         d = lax.rem(me + j, devices)
         t2, s2 = d // slabs, lax.rem(d, slabs)
         return pltpu.make_async_remote_copy(
-            last.at[:, 1 + s2 * depth + z, xrow(t2, row, PAD), :],
-            back.at[me, :, z, pl.ds(row, rows), :],
+            last.at[:, pl.ds(1 + s2 * depth, depth), xrow(ch, t2, LOW), :],
+            back.at[me, :, :, kept(ch), :],
             s_d, r_d.at[ch], device_id=(t2, s2), device_id_type=MESH)
 
-    def start_d(ch, c):
-        lax.fori_loop(1, devices, lambda j, c: (d_copy(ch, j).start(), c)[1], 0)
-        return c
-
-    lax.fori_loop(0, chunks, start_d, 0)
-    own_d = pltpu.make_async_copy(
-        last.at[:, pl.ds(1 + s * depth, depth), pl.ds(pl.multiple_of(PAD + t * xb, 8), xb), :],
-        back.at[me], loc.at[4])
-    own_d.start()
-    own_d.wait()
+    def own_d(ch):
+        return pltpu.make_async_copy(
+            last.at[:, pl.ds(1 + s * depth, depth), xrow(ch, t, LOW), :],
+            back.at[me, :, :, kept(ch), :], loc.at[3, 0, ch])
+
+    def others(ch):
+        return hat.at[pl.ds(0, devices - 1), :, :, kept(ch), :]
+
+    for c in range(chunks + 1):
+        if c < chunks:
+            own_b(c).wait()
+            wait_bytes(others(c), r_b.at[c])
+        for j in range(SWEEPS):
+            tile(c, j, xstep if c < chunks else LOW)
+        if c > 0:
+            lax.fori_loop(1, devices, lambda j, k, c=c: (d_copy(c - 1, j).start(), k)[1], 0)
+            own_d(c - 1).start()
     shrink = [math.exp(-math.log(ALPHA) * n / steps) / steps for n in range(steps)]
 
     def f_copy(arr, ch, j):
-        z, row = at_chunk(ch)
         t2 = lax.rem(t + j, groups)
         ref = so_ref if arr == 0 else ao_ref
         return pltpu.make_async_remote_copy(
-            outs.at[arr, pl.ds(t2 * local, local), z, pl.ds(row, rows), :],
-            ref.at[:, z, xrow(t, row), :],
+            outs.at[arr, pl.ds(t2 * local, local), :, kept(ch), :],
+            ref.at[:, :, xrow(ch, t), :],
             s_f.at[ch, arr, j - 1], r_f.at[ch, arr, j - 1],
             device_id=(t2, s), device_id_type=MESH)
 
+    def own_f(arr, ch):
+        ref = so_ref if arr == 0 else ao_ref
+        return pltpu.make_async_copy(
+            outs.at[arr, pl.ds(t * local, local), :, kept(ch), :],
+            ref.at[:, :, xrow(ch, t), :], loc.at[4, arr, ch])
+
     def backward(ch, c):
-        z, row = at_chunk(ch)
-        got = back.at[pl.ds(0, devices - 1), :, z, pl.ds(row, rows), :]
-        pltpu.make_async_copy(got, got, r_d.at[ch]).wait()
-
-        def piece(r, c):
-            at = pl.ds(pl.multiple_of(row + r * 8, 8), 8)
+        wait_bytes(others(ch), r_d.at[ch])
+        own_d(ch).wait()
+
+        def piece(z, c):
+            at = kept(ch)
 
             def load(k):
                 return back[k, 0, z, at, :], back[k, 1, z, at, :]
@@ -426,34 +450,29 @@
                 outs[1, steps - 1 - n, z, at, :] = im * shrink[n]
             return c
 
-        lax.fori_loop(0, rows // 8, piece, 0)
-        for j in range(1, groups):
-            for arr in range(2):
+        lax.fori_loop(0, depth, piece, 0)
+        for arr in range(2):
+            for j in range(1, groups):
                 f_copy(arr, ch, j).start()
+            own_f(arr, ch).start()
         return c
 
     lax.fori_loop(0, chunks, backward, 0)
-    own_f = [
-        pltpu.make_async_copy(
-            outs.at[arr, pl.ds(t * local, local)], ref.at[:, :, mine, :], loc.at[5 + arr])
-        for arr, ref in enumerate((so_ref, ao_ref))
-    ]
-    for c in own_f:
-        c.start()
-    for c in own_f:
-        c.wait()
-
     def finish(ch, c):
         for j in range(1, groups):
             for arr in range(2):
                 a_copy(arr, ch, j).wait_send()
                 f_copy(arr, ch, j).wait()
+        for arr in range(2):
+            own_f(arr, ch).wait()
         return c
 
     lax.fori_loop(0, chunks, finish, 0)
-    pltpu.make_async_copy(most, most, s_b).wait()
-    pltpu.make_async_copy(most, most, s_d).wait()
-    pltpu.make_async_copy(many, many, s_r).wait()
+    most = hat.at[pl.ds(0, devices - 1)]
+    wait_bytes(most, s_b)
+    wait_bytes(most, s_d)
+    wait_bytes(planes_of(slabs // 2 - 1), s_r)
+    wait_bytes(planes_of(slabs // 2), s_y)
 
 
 def fused_body(state_rhs, adjoint_rhs, reaction):
@@ -461,7 +480,8 @@
     local, depth, nx, ny = state_rhs.shape
     dims = (groups, slabs, local, depth, nx, ny)
     steps, devices, nz, xb = groups * local, groups * slabs, depth * slabs, nx // groups
-    chunks = depth * 2
+    chunks = xb // 8
+    edged = LOW + nx + HIGH
     turn = 2.0 * math.pi * np.arange(steps) / steps
     rate = ALPHA ** (1.0 / steps)
     lam = np.stack((1.0 - rate * np.cos(turn), rate * np.sin(turn)), axis=1).astype(np.float32)
@@ -477,17 +497,17 @@
         scratch_shapes=[
             pltpu.VMEM((2, steps, depth, xb, ny), f32),
             pltpu.VMEM((devices, 2, depth, xb, ny), f32),
-            pltpu.VMEM((2, nz, nx, ny), f32),
+            pltpu.VMEM((2, nz, edged, ny), f32),
             pltpu.VMEM((nz, nx, ny), f32),
-            pltpu.VMEM((2, nz, nx, ny), f32),
-            pltpu.VMEM((2, nz + 2, nx + 2 * PAD, ny), f32),
-            pltpu.VMEM((2, nz + 2, nx + 2 * PAD, ny), f32),
+            pltpu.VMEM((2, nz, edged, ny), f32),
+            pltpu.VMEM((2, nz + 2, edged, ny), f32),
+            pltpu.VMEM((2, nz + 2, edged, ny), f32),
             pltpu.VMEM((devices, 2, depth, xb, ny), f32),
             pltpu.VMEM((2, steps, depth, xb, ny), f32),
             dma((chunks, 2, groups - 1)),
             dma((chunks, 2, groups - 1)),
             dma,
-            dma,
+            dma((chunks,)),
             dma,
             dma((chunks,)),
             dma((chunks, 2, groups - 1)),
@@ -496,7 +516,9 @@
             dma,
             dma,
             dma,
-            dma((7,)),
+            dma,
+            dma,
+            dma((5, 2, chunks)),
         ],
         compiler_params=pltpu.CompilerParams(
             has_side_effects=True, vmem_limit_bytes=58 * 1024 * 1024
@@ -512,7 +534,8 @@
     def chosen(state_rhs, adjoint_rhs, reaction):
         steps = state_rhs.shape[0] * groups
         fits = steps == groups * slabs and steps & (steps - 1) == 0 and groups % 2 == 0
-        fits = fits and state_rhs.shape[2] % (16 * groups) == 0 and state_rhs.shape[3] == 128
+        fits = fits and slabs % 2 == 0 and slabs > 2 and state_rhs.shape[3] % 128 == 0
+        fits = fits and state_rhs.shape[2] % (8 * groups) == 0 and SWEEPS <= LOW <= 8 * groups
         return (fused_body if fits else body)(state_rhs, adjoint_rhs, reaction)
 
     return jax.shard_map(chosen, mesh=mesh, in_specs=in_specs, out_specs=out_specs, check_vma=False)

time: 155 us -> 133 us (0.86)
  Pallas kernels: 150 us -> 129 us
    pallas_call x1, Pallas kernels: 150 us -> 129 us  [fused_body(): pl.pallas_call(functools.partial(whole_kernel, dims), out_shape=(shape, s...]
where the time goes in v2:
time: 133 us
  Pallas kernels  129 us (97%)
  local copies, waits for them, and re-layouts  3.36 us (3%)
    pallas_call x1, Pallas kernels, fused_body(): pl.pallas_call(functools.partial(whole_kernel, dims), out_shape=(shape, s...  129 us
    unnamed x4, local copies, waits for them, and re-layouts  3.36 us

profile of v2, /device:TPU:0, one launch (start us, length us, event | category | flops | bytes accessed | tf_op | source)
XLA Modules:
  0.0 132.9 jit_solution(13276717636566261759)
XLA Ops:
  0.6 128.9 %shard_map.59 = (f32[8,2,128,128]{3,2,1,0:T(8,128)}, f32[8,2,128,128]{3,2,1,0:T(8,128)}) custom-call(f32[32,2]{1,0:T(8,128)} %constant.2.clone.lam_ref, f32[8,2,128,128]{3,2,1,0:T(8,128)} %s_ref.1, f32[8,2,128,128]{3,2,1,0:T(8,128)} %a_ref.1, f32[2,128,128]{2,1,0:T(8,128)} %re_ref.1), custom_call_target="tpu_custom_call" | custom-call | tf_op jit(solution)/shard_map/pallas_call | solution.py:492
  129.5 0.0 copy-start
  129.5 2.4 %copy.8 = f32[8,2,128,128]{3,2,1,0:T(8,128)} copy(f32[8,2,128,128]{3,2,1,0:T(8,128)} %get-tuple-element.4) | data formatting | bytes 2097152
  131.9 0.0 copy-done
  131.9 1.0 copy.9
Async XLA Ops:
  129.5 2.4 %copy-start = (f32[8,2,128,128]{3,2,1,0:T(8,128)S(1)}, f32[8,2,128,128]{3,2,1,0:T(8,128)}, u32[]{:S(2)}) copy-start(f32[8,2,128,128]{3,2,1,0:T(8,128)} %get-tuple-element.5) | copy-start | bytes 3145732

commit v3 on v2

--- a/solution.py
+++ b/solution.py
@@ -225,6 +225,17 @@
     part = lax.rem(t, 2)
     partner = t + 1 - 2 * part
 
+    bits = devices.bit_length() - 1
+    order = sorted(range(1, devices), key=lambda j: (-((j >> 2) & 1), -((j >> 1) & 1), -((j >> 4) & 1), -j))
+    flip = [lax.rem(me // (1 << b), 2) for b in range(bits)]
+
+    def across(j):
+        d = me
+        for b in range(bits):
+            if (j >> b) & 1:
+                d = d + (1 << b) * (1 - 2 * flip[b])
+        return d
+
     def kept(ch):
         return pl.ds(pl.multiple_of(ch * rows, rows), rows)
 
@@ -307,7 +318,7 @@
     growth = [math.exp(math.log(ALPHA) * n / steps) for n in range(steps)]
 
     def b_copy(ch, j):
-        d = lax.rem(me + j, devices)
+        d = across(j)
         return pltpu.make_async_remote_copy(
             hat.at[d, :, :, kept(ch), :],
             src.at[:, pl.ds(s * depth, depth), xrow(ch, t, LOW), :],
@@ -335,7 +346,8 @@
             return c
 
         lax.fori_loop(0, depth, piece, 0)
-        lax.fori_loop(1, devices, lambda j, c: (b_copy(ch, j).start(), c)[1], 0)
+        for j in order:
+            b_copy(ch, j).start()
         own_b(ch).start()
         return c
 
@@ -394,7 +406,7 @@
     last = u0 if SWEEPS % 2 else u1
 
     def d_copy(ch, j):
-        d = lax.rem(me + j, devices)
+        d = across(j)
         t2, s2 = d // slabs, lax.rem(d, slabs)
         return pltpu.make_async_remote_copy(
             last.at[:, pl.ds(1 + s2 * depth, depth), xrow(ch, t2, LOW), :],
@@ -416,7 +428,8 @@
         for j in range(SWEEPS):
             tile(c, j, xstep if c < chunks else LOW)
         if c > 0:
-            lax.fori_loop(1, devices, lambda j, k, c=c: (d_copy(c - 1, j).start(), k)[1], 0)
+            for j in order:
+                d_copy(c - 1, j).start()
             own_d(c - 1).start()
     shrink = [math.exp(-math.log(ALPHA) * n / steps) / steps for n in range(steps)]
 

time: 133 us -> 132 us (level)
  no operation moved by 1% of the time
where the time goes in v3:
time: 132 us
  Pallas kernels  128 us (97%)
  local copies, waits for them, and re-layouts  3.36 us (3%)
    pallas_call x1, Pallas kernels, fused_body(): pl.pallas_call(functools.partial(whole_kernel, dims), out_shape=(shape, s...  128 us
    unnamed x4, local copies, waits for them, and re-layouts  3.36 us

profile of v3, /device:TPU:0, one launch (start us, length us, event | category | flops | bytes accessed | tf_op | source)
XLA Modules:
  0.0 131.8 jit_solution(3011420498700636356)
XLA Ops:
  0.6 127.8 %shard_map.59 = (f32[8,2,128,128]{3,2,1,0:T(8,128)}, f32[8,2,128,128]{3,2,1,0:T(8,128)}) custom-call(f32[32,2]{1,0:T(8,128)} %constant.2.clone.lam_ref, f32[8,2,128,128]{3,2,1,0:T(8,128)} %s_ref.1, f32[8,2,128,128]{3,2,1,0:T(8,128)} %a_ref.1, f32[2,128,128]{2,1,0:T(8,128)} %re_ref.1), custom_call_target="tpu_custom_call" | custom-call | tf_op jit(solution)/shard_map/pallas_call | solution.py:505
  128.4 0.0 copy-start
  128.4 2.4 %copy.8 = f32[8,2,128,128]{3,2,1,0:T(8,128)} copy(f32[8,2,128,128]{3,2,1,0:T(8,128)} %get-tuple-element.4) | data formatting | bytes 2097152
  130.8 0.0 copy-done
  130.8 1.0 copy.9
Async XLA Ops:
  128.4 2.4 %copy-start = (f32[8,2,128,128]{3,2,1,0:T(8,128)S(1)}, f32[8,2,128,128]{3,2,1,0:T(8,128)}, u32[]{:S(2)}) copy-start(f32[8,2,128,128]{3,2,1,0:T(8,128)} %get-tuple-element.5) | copy-start | bytes 3145732
